TPU v7x, 8 devices: a whole 2x2x1 slice. The times are simulated.
8 devices in a mesh: dp: 1 (over z), tp: 8 (over x, y, core).
Axes of the slice: x: 2, y: 2, z: 1, core: 2. Of those that a mesh axis runs over, the one named last changes fastest.
Arguments:
- x: bfloat16 [2048, 12288], P('dp')
- w_gate: bfloat16 [12288, 33792], P(None, 'tp')
- w_up: bfloat16 [12288, 33792], P(None, 'tp')
- w_down: bfloat16 [33792, 12288], P('tp')
Outputs:
- output: bfloat16 [2048, 12288], P('dp')
All inputs are finite; a program needn't handle non-finite values.
Results may differ from a plain program's by a relative error of at most 0.016.
Values are sent between devices in bfloat16 or wider.
A program may use at most 2 GiB of HBM per device.

v0:
```python
import jax
import jax.numpy as jnp
from jax import lax
from jax.sharding import PartitionSpec as P


def solution(mesh):
    def step(x, w_gate, w_up, w_down):
        gate = jnp.dot(x, w_gate, preferred_element_type=jnp.float32)
        up = jnp.dot(x, w_up, preferred_element_type=jnp.float32)
        hidden = (jax.nn.silu(gate) * up).astype(jnp.bfloat16)
        term = jnp.dot(hidden, w_down, preferred_element_type=jnp.float32).astype(jnp.bfloat16)
        return lax.psum(term, "tp")

    return jax.shard_map(
        step,
        mesh=mesh,
        in_specs=(P("dp", None), P(None, "tp"), P(None, "tp"), P("tp", None)),
        out_specs=P("dp", None),
        check_vma=False,
    )
```

profile of v0, /device:TPU:0, one launch (start us, length us, event | category | flops | bytes accessed | tf_op | source)
XLA Modules:
  0.0 1344.4 jit_solution(11108140767932615519)
XLA Ops:
  6.5 0.0 all-reduce.2.cloned.1.call-start
  6.5 236.8 %fusion = f32[2048,4224]{1,0:T(8,128)} fusion(bf16[2048,12288]{1,0:T(8,128)(2,1)} %param.4, bf16[12288,4224]{1,0:T(8,128)(2,1)} %param.5), kind=kOutput, calls=%fused_computation.2 | convolution fusion | flops 212600881152 | bytes 188743680 | tf_op jit(solution)/shard_map/dot_general | solution.py:9
  243.3 255.4 %multiply_convert_fusion = bf16[2048,4224]{1,0:T(8,128)(2,1)} fusion(f32[2048,4224]{1,0:T(8,128)} %fusion, bf16[2048,12288]{1,0:T(8,128)(2,1)} %param.4, bf16[12288,4224]{1,0:T(8,128)(2,1)} %param.6), kind=kOutput, calls=%fused_computation.1 | convolution fusion | flops 212652785664 | bytes 206045184 | tf_op jit(solution)/shard_map/dot_general | solution.py:10
  498.7 234.9 %convolution_convert_fusion = bf16[2048,12288]{1,0:T(8,128)(2,1)} fusion(bf16[2048,4224]{1,0:T(8,128)(2,1)} %multiply_convert_fusion, bf16[4224,12288]{1,0:T(8,128)(2,1)} %param.7), kind=kOutput, calls=%fused_computation | convolution fusion | flops 212626046976 | bytes 171442176 | tf_op jit(solution)/shard_map/dot_general | solution.py:12
  733.7 0.0 all-reduce.2.cloned.1.call-update
  733.7 570.2 %all-reduce.2.cloned.1.call-done = bf16[2048,12288]{1,0:T(8,128)(2,1)} async-done(((bf16[2048,12288]{1,0:T(8,128)(2,1)}), bf16[2048,12288]{1,0:T(8,128)(2,1)}) %all-reduce.2.cloned.1.call-update) | async-done | bytes 50331664 | tf_op jit(solution)/shard_map/psum | solution.py:13
  1303.9 33.7 %copy.6 = bf16[2048,12288]{1,0:T(8,128)(2,1)} copy(bf16[2048,12288]{1,0:T(8,128)(2,1)} %all-reduce.2.cloned.1.call-done) | data formatting | bytes 100663296
Async XLA Ops:
  6.5 1297.3 %all-reduce.2.cloned.1.call-start = ((), (), s32[]{:S(2)}) async-start(), calls=%async_computation | async-start | bytes 100663296 | tf_op jit(solution)/shard_map/psum | solution.py:13
Sparse Core Ops, SparseCore 0:
  733.8 569.9 all-reduce.1
where the time goes:
time: 1340 us
  matrix products  727 us (54%)
  waiting for transfers between devices  570 us (43%)
  local copies, waits for them, and re-layouts  33.7 us (3%)
  between operations  13.4 us (1%)
    psum x1, waiting for transfers between devices, step(): return lax.psum(term, 'tp')  570 us
    dot_general x1, matrix products, step(): up = jnp.dot(x, w_up, preferred_element_type=jnp.float32)  255 us
    dot_general x1, matrix products, step(): gate = jnp.dot(x, w_gate, preferred_element_type=jnp.float32)  237 us
    dot_general x1, matrix products, step(): jnp.dot(hidden, w_down, preferred_element_type=jnp.float32)  235 us
    unnamed x1, local copies, waits for them, and re-layouts  33.7 us
  transfers between devices with their start and end apart: 1, of which 1 were waited for; matrix products, arithmetic and copies ran while one was open for 0% of the time, Pallas kernels for 0%

commit v1 on v0

v1 whole, which is shorter than its diff:
```python
import functools

import jax
import jax.numpy as jnp
from jax import lax
from jax.experimental import pallas as pl
from jax.experimental.pallas import tpu as pltpu
from jax.sharding import PartitionSpec as P

MESH = pl.DeviceIdType.MESH
F32, BF16 = jnp.float32, jnp.bfloat16

BM = 512
GC = 128
DC = 1024
NB = 4
H0, H1, H2 = BM // 2, BM // 4, BM // 8


def kernel(x_hbm, wg_hbm, wu_hbm, wd_hbm, y_hbm, x_v, w_v, h_v, d_v, keep, out0, in0, out1, in1, out2, in2, fin,
           x_sem, w_sem, d_sem, s_sem, r_sem, f_sem):
    rows, ff = x_hbm.shape[0], wg_hbm.shape[1]
    chunks, ng, nd = rows // BM, ff // GC, y_hbm.shape[1] // DC
    tiles, gates = chunks * nd, chunks * ng

    me = lax.axis_index("tp")
    core, cy, cx = me % 2, (me // 2) % 2, me // 4
    partner = me + 1 - 2 * core
    ny, nx = me + 2 - 4 * cy, me + 4 - 8 * cx

    def x_load(c):
        return pltpu.make_async_copy(x_hbm.at[pl.ds(c * BM, BM)], x_v, x_sem)

    def w_load(i):
        slot = i % 2
        cols = pl.ds(pl.multiple_of((i % ng) * GC, GC), GC)
        return (
            pltpu.make_async_copy(wg_hbm.at[:, cols], w_v.at[slot, :, pl.ds(0, GC)], w_sem.at[slot, 0]),
            pltpu.make_async_copy(wu_hbm.at[:, cols], w_v.at[slot, :, pl.ds(GC, GC)], w_sem.at[slot, 1]),
        )

    def d_load(t):
        slot = t % 2
        cols = pl.ds(pl.multiple_of((t % nd) * DC, DC), DC)
        return pltpu.make_async_copy(wd_hbm.at[:, cols], d_v.at[slot], d_sem.at[slot])

    def place(t):
        turn = t % 2
        first = cx * (1 - turn) + cy * turn
        second = cy * (1 - turn) + cx * turn
        n1 = nx * (1 - turn) + ny * turn
        n2 = ny * (1 - turn) + nx * turn
        return t % NB, first, second, n1, n2

    def remote(src, dst, stage, slot, to):
        return pltpu.make_async_remote_copy(
            src_ref=src, dst_ref=dst, send_sem=s_sem.at[stage, slot], recv_sem=r_sem.at[stage, slot],
            device_id={"tp": to}, device_id_type=MESH,
        )

    def y_at(t, offset, size):
        row = (t // nd) * BM + offset
        return y_hbm.at[pl.ds(pl.multiple_of(row, size), size), pl.ds(pl.multiple_of((t % nd) * DC, DC), DC)]

    def send(t, stage):
        slot, first, second, n1, n2 = place(t)
        if stage == 0:
            return remote(out0.at[slot], in0.at[slot], 0, slot, partner)
        if stage == 1:
            return remote(out1.at[slot], in1.at[slot], 1, slot, n1)
        if stage == 2:
            return remote(out2.at[slot], in2.at[slot], 2, slot, n2)
        if stage == 3:
            block = y_at(t, core * H0 + first * H1 + second * H2, H2)
            return remote(fin.at[slot], block, 3, slot, n2)
        if stage == 4:
            block = y_at(t, core * H0 + first * H1, H1)
            return remote(block, block, 4, slot, n1)
        block = y_at(t, core * H0, H0)
        return remote(block, block, 5, slot, partner)

    def own(t):
        slot, first, second, _, _ = place(t)
        return pltpu.make_async_copy(fin.at[slot], y_at(t, core * H0 + first * H1 + second * H2, H2), f_sem.at[slot])

    def at(base, size):
        return pl.ds(pl.multiple_of(base, size), size)

    def advance(t, n):
        slot, first, second, _, _ = place(t)
        send(t, n - 1).wait()
        if n == 1:
            mine, theirs = at(first * H1, H1), at((1 - first) * H1, H1)
            out1[slot] = (keep[slot, theirs, :] + in0[slot, theirs, :].astype(F32)).astype(BF16)
            keep[slot, mine, :] = keep[slot, mine, :] + in0[slot, mine, :].astype(F32)
            send(t, 1).start()
        elif n == 2:
            mine, theirs = at(first * H1 + second * H2, H2), at(first * H1 + (1 - second) * H2, H2)
            out2[slot] = (keep[slot, theirs, :] + in1[slot, at((1 - second) * H2, H2), :].astype(F32)).astype(BF16)
            keep[slot, mine, :] = keep[slot, mine, :] + in1[slot, at(second * H2, H2), :].astype(F32)
            send(t, 2).start()
        elif n == 3:
            mine = at(first * H1 + second * H2, H2)
            fin[slot] = (keep[slot, mine, :] + in2[slot].astype(F32)).astype(BF16)
            send(t, 3).start()
            own(t).start()
        elif n == 4:
            own(t).wait()
            send(t, 4).start()
        elif n == 5:
            send(t, 5).start()

    def tick(t, guard):
        for n in range(6, 0, -1):
            if guard:
                pl.when(t >= n)(functools.partial(advance, t - n, n))
            else:
                advance(t - n, n)

    def gate_step(c, g):
        i = c * ng + g

        @pl.when(g == 0)
        def _():
            x_load(c).wait()

        for copy in w_load(i):
            copy.wait()

        @pl.when(i + 1 < gates)
        def _():
            for copy in w_load(i + 1):
                copy.start()

        both = jnp.dot(x_v[...], w_v[i % 2], preferred_element_type=F32)
        gate, up = both[:, :GC], both[:, GC:]
        h_v[c % 2, :, pl.ds(pl.multiple_of(g * GC, GC), GC)] = (jax.nn.silu(gate) * up).astype(BF16)

        @pl.when((g == ng - 1) & (c + 1 < chunks))
        def _():
            x_load(c + 1).start()

    def down_step(t, guard):
        c, slot = t // nd, t % NB
        d_load(t).wait()

        @pl.when(t + 1 < tiles)
        def _():
            d_load(t + 1).start()

        tick(t, guard)
        theirs, mine = at((1 - core) * H0, H0), at(core * H0, H0)
        out0[slot] = jnp.dot(h_v[c % 2, theirs, :], d_v[t % 2], preferred_element_type=F32).astype(BF16)
        keep[slot] = jnp.dot(h_v[c % 2, mine, :], d_v[t % 2], preferred_element_type=F32)
        send(t, 0).start()

    x_load(0).start()
    for copy in w_load(0):
        copy.start()
    d_load(0).start()

    barrier = pltpu.get_barrier_semaphore()
    for other in (partner, nx, ny):
        pl.semaphore_signal(barrier, inc=1, device_id={"tp": other}, device_id_type=MESH)
    pl.semaphore_wait(barrier, 3)

    @pl.loop(0, ng)
    def _(g):
        gate_step(0, g)

    @pl.loop(0, tiles - nd)
    def _(t):
        c, d = t // nd + 1, t % nd

        @pl.loop(d * ng // nd, (d + 1) * ng // nd)
        def _(g):
            gate_step(c, g)

        down_step(t, True)

    @pl.loop(tiles - nd, tiles)
    def _(t):
        down_step(t, False)

    for t in range(tiles, tiles + 6):
        for n in range(6, 0, -1):
            if 0 <= t - n < tiles:
                advance(t - n, n)


def solution(mesh):
    def step(x, w_gate, w_up, w_down):
        rows, d = x.shape
        ff = w_gate.shape[1]
        dma = pltpu.SemaphoreType.DMA
        return pl.pallas_call(
            kernel,
            out_shape=jax.ShapeDtypeStruct((rows, d), BF16),
            in_specs=[pl.BlockSpec(memory_space=pl.ANY)] * 4,
            out_specs=pl.BlockSpec(memory_space=pl.ANY),
            scratch_shapes=[
                pltpu.VMEM((BM, d), BF16),
                pltpu.VMEM((2, d, 2 * GC), BF16),
                pltpu.VMEM((2, BM, ff), BF16),
                pltpu.VMEM((2, ff, DC), BF16),
                pltpu.VMEM((NB, H0, DC), F32),
                pltpu.VMEM((NB, H0, DC), BF16),
                pltpu.VMEM((NB, H0, DC), BF16),
                pltpu.VMEM((NB, H1, DC), BF16),
                pltpu.VMEM((NB, H1, DC), BF16),
                pltpu.VMEM((NB, H2, DC), BF16),
                pltpu.VMEM((NB, H2, DC), BF16),
                pltpu.VMEM((NB, H2, DC), BF16),
                dma,
                dma((2, 2)),
                dma((2,)),
                dma((6, NB)),
                dma((6, NB)),
                dma((NB,)),
            ],
            compiler_params=pltpu.CompilerParams(
                collective_id=0, has_side_effects=True, vmem_limit_bytes=67_043_328
            ),
            cost_estimate=pl.CostEstimate(
                flops=6 * rows * d * ff, bytes_accessed=2 * (rows // BM * 3 * d * ff + 4 * rows * d), transcendentals=rows * ff
            ),
            name="mlp",
        )(x, w_gate, w_up, w_down)

    return jax.shard_map(
        step,
        mesh=mesh,
        in_specs=(P("dp", None), P(None, "tp"), P(None, "tp"), P("tp", None)),
        out_specs=P("dp", None),
        check_vma=False,
    )
```

time: 1340 us -> 831 us (0.62)
  Pallas kernels: 0 us -> 797 us
  matrix products: 727 us -> 0 us
  waiting for transfers between devices: 570 us -> 0 us
    pallas_call x0 -> x1, Pallas kernels: none -> 797 us  [step(): pl.pallas_call(kernel, out_shape=jax.ShapeDtypeStruct((rows, d), BF16), i...]
    dot_general x3 -> x0, matrix products: 727 us -> none  [the longest x1 255 us: step(): up = jnp.dot(x, w_up, preferred_element_type=jnp.float32)]
    psum x1 -> x0, waiting for transfers between devices: 570 us -> none  [step(): return lax.psum(term, 'tp')]
  transfers between devices with their start and end apart: 1 -> 0, of which waited for: 1 -> 0; matrix products, arithmetic and copies ran while one was open for 0% -> 0% of each run, Pallas kernels for 0% -> 0%
where the time goes in v1:
time: 831 us
  Pallas kernels  797 us (96%)
  local copies, waits for them, and re-layouts  33.7 us (4%)
    pallas_call x1, Pallas kernels, step(): pl.pallas_call(kernel, out_shape=jax.ShapeDtypeStruct((rows, d), BF16), i...  797 us
    unnamed x1, local copies, waits for them, and re-layouts  33.7 us

profile of v1, /device:TPU:0, one launch (start us, length us, event | category | flops | bytes accessed | tf_op | source)
XLA Modules:
  0.0 830.6 jit_solution(1169606466863076240)
XLA Ops:
  0.0 796.8 %mlp.1 = bf16[2048,12288]{1,0:T(8,128)(2,1)} custom-call(bf16[2048,12288]{1,0:T(8,128)(2,1)} %x_hbm.1, bf16[12288,4224]{1,0:T(8,128)(2,1)} %wg_hbm.1, bf16[12288,4224]{1,0:T(8,128)(2,1)} %wu_hbm.1, bf16[4224,12288]{1,0:T(8,128)(2,1)} %wd_hbm.1), custom_call_target="tpu_custom_call" | custom-call | flops 637802643456 | bytes 1447034880 | tf_op jit(solution)/shard_map/mlp/pallas_call | solution.py:196
  796.8 33.7 %copy.6 = bf16[2048,12288]{1,0:T(8,128)(2,1)} copy(bf16[2048,12288]{1,0:T(8,128)(2,1)} %mlp.1) | data formatting | bytes 100663296

commit v2 on v1

v2 whole, which is shorter than its diff:
```python
import functools

import jax
import jax.numpy as jnp
from jax import lax
from jax.experimental import pallas as pl
from jax.experimental.pallas import tpu as pltpu
from jax.sharding import PartitionSpec as P

MESH = pl.DeviceIdType.MESH
F32, BF16 = jnp.float32, jnp.bfloat16

TM, GC, DC = 256, 128, 768
BM = 2 * TM
NB = 8
NW = 3
H0, H1, H2 = TM // 2, TM // 4, TM // 8


def kernel(x_hbm, wg_hbm, wu_hbm, wd_hbm, y_hbm, x_v, w_v, h_v, d_v, keep, out0, in0, out1, in1, out2, in2, fin,
           x_sem, w_sem, d_sem, s_sem, r_sem, f_sem):
    rows, ff = x_hbm.shape[0], wg_hbm.shape[1]
    ng, nd = ff // GC, y_hbm.shape[1] // DC
    wide = (rows - 2 * TM) // BM
    gates, downs = (wide + 2) * ng, (wide + 2) * nd
    edge, tiles = nd * (1 + 2 * wide), nd * (2 + 2 * wide)

    me = lax.axis_index("tp")
    core, cy, cx = me % 2, (me // 2) % 2, me // 4
    partner = me + 1 - 2 * core
    ny, nx = me + 2 - 4 * cy, me + 4 - 8 * cx

    def at(base, size):
        return pl.ds(pl.multiple_of(base, size), size)

    def x_load(c, size):
        base = jnp.where(c == 0, 0, TM + (c - 1) * BM)
        return pltpu.make_async_copy(x_hbm.at[at(base, TM) if size == TM else pl.ds(pl.multiple_of(base, TM), BM)],
                                     x_v.at[pl.ds(0, size)], x_sem)

    def w_load(i):
        slot = i % NW
        cols = at((i % ng) * GC, GC)
        return (
            pltpu.make_async_copy(wg_hbm.at[:, cols], w_v.at[slot, :, pl.ds(0, GC)], w_sem.at[slot, 0]),
            pltpu.make_async_copy(wu_hbm.at[:, cols], w_v.at[slot, :, pl.ds(GC, GC)], w_sem.at[slot, 1]),
        )

    def d_load(t):
        slot = t % 2
        return pltpu.make_async_copy(wd_hbm.at[:, at((t % nd) * DC, DC)], d_v.at[slot], d_sem.at[slot])

    def place(u):
        turn = u % 2
        first = cx * (1 - turn) + cy * turn
        second = cy * (1 - turn) + cx * turn
        n1 = nx * (1 - turn) + ny * turn
        n2 = ny * (1 - turn) + nx * turn
        return u % NB, first, second, n1, n2

    def remote(src, dst, stage, slot, to):
        return pltpu.make_async_remote_copy(
            src_ref=src, dst_ref=dst, send_sem=s_sem.at[stage, slot], recv_sem=r_sem.at[stage, slot],
            device_id={"tp": to}, device_id_type=MESH,
        )

    def y_at(u, offset, size):
        v = jnp.clip(u - nd, 0, 2 * wide * nd - 1)
        t = v // 2
        row = jnp.where(u < nd, 0, jnp.where(u >= edge, rows - TM, TM + (t // nd) * BM + (v % 2) * TM))
        col = jnp.where((u < nd) | (u >= edge), u % nd, t % nd)
        return y_hbm.at[at(row + offset, size), at(col * DC, DC)]

    def send(u, stage):
        slot, first, second, n1, n2 = place(u)
        if stage == 0:
            return remote(out0.at[slot], in0.at[slot], 0, slot, partner)
        if stage == 1:
            return remote(out1.at[slot], in1.at[slot], 1, slot, n1)
        if stage == 2:
            return remote(out2.at[slot], in2.at[slot], 2, slot, n2)
        if stage == 3:
            block = y_at(u, core * H0 + first * H1 + second * H2, H2)
            return remote(fin.at[slot], block, 3, slot, n2)
        if stage == 4:
            block = y_at(u, core * H0 + first * H1, H1)
            return remote(block, block, 4, slot, n1)
        block = y_at(u, core * H0, H0)
        return remote(block, block, 5, slot, partner)

    def own(u):
        slot, first, second, _, _ = place(u)
        return pltpu.make_async_copy(fin.at[slot], y_at(u, core * H0 + first * H1 + second * H2, H2), f_sem.at[slot])

    def arrived(u, n):
        send(u, n - 1).wait()
        if n == 4:
            own(u).wait()

    def add(u, n):
        slot, first, second, _, _ = place(u)
        if n == 1:
            mine, theirs = at(first * H1, H1), at((1 - first) * H1, H1)
            out1[slot] = (keep[slot, theirs, :] + in0[slot, theirs, :].astype(F32)).astype(BF16)
            keep[slot, mine, :] = keep[slot, mine, :] + in0[slot, mine, :].astype(F32)
        elif n == 2:
            mine, theirs = at(first * H1 + second * H2, H2), at(first * H1 + (1 - second) * H2, H2)
            out2[slot] = (keep[slot, theirs, :] + in1[slot, at((1 - second) * H2, H2), :].astype(F32)).astype(BF16)
            keep[slot, mine, :] = keep[slot, mine, :] + in1[slot, at(second * H2, H2), :].astype(F32)
        elif n == 3:
            mine = at(first * H1 + second * H2, H2)
            fin[slot] = (keep[slot, mine, :] + in2[slot].astype(F32)).astype(BF16)

    def forward(u, n):
        if n < 6:
            send(u, n).start()
        if n == 3:
            own(u).start()

    def tick(u, stages=range(6, 0, -1)):
        for part in (arrived, add, forward):
            for n in stages:
                part(u - 2 * n, n)

    def tick_if(u):
        def one(n):
            for part in (arrived, add, forward):
                part(u - 2 * n, n)

        for n in range(6, 0, -1):
            pl.when(u >= 2 * n)(functools.partial(one, n))

    def gate_step(c, g, size, ticked=None):
        i = c * ng + g

        @pl.when(g == 0)
        def _():
            x_load(c, size).wait()

        for copy in w_load(i):
            copy.wait()

        @pl.when(i + NW - 1 < gates)
        def _():
            for copy in w_load(i + NW - 1):
                copy.start()

        if ticked is not None:
            tick(ticked)
        both = jnp.dot(x_v[pl.ds(0, size), :], w_v[i % NW], preferred_element_type=F32)
        gate, up = both[:, :GC], both[:, GC:]
        h_v[c % 2, pl.ds(0, size), at(g * GC, GC)] = (jax.nn.silu(gate) * up).astype(BF16)

    def down_step(t, c, u, size, before):
        d_load(t).wait()

        @pl.when(t + 1 < downs)
        def _():
            d_load(t + 1).start()

        before()
        for k in range(size // TM):
            slot = (u + k) % NB
            theirs, mine = at(k * TM + (1 - core) * H0, H0), at(k * TM + core * H0, H0)
            out0[slot] = jnp.dot(h_v[c % 2, theirs, :], d_v[t % 2], preferred_element_type=F32).astype(BF16)
            keep[slot] = jnp.dot(h_v[c % 2, mine, :], d_v[t % 2], preferred_element_type=F32)
        for k in range(size // TM):
            send(u + k, 0).start()

    def span(d):
        return d * ng // nd, (d + 1) * ng // nd

    x_load(0, TM).start()
    for i in range(NW - 1):
        for copy in w_load(i):
            copy.start()
    d_load(0).start()

    barrier = pltpu.get_barrier_semaphore()
    for other in (partner, nx, ny):
        pl.semaphore_signal(barrier, inc=1, device_id={"tp": other}, device_id_type=MESH)
    pl.semaphore_wait(barrier, 3)

    @pl.loop(0, ng)
    def _(g):
        gate_step(0, g, TM)

    x_load(1, BM).start()

    @pl.loop(0, nd)
    def _(t):
        down_step(t, 0, t, TM, lambda: tick_if(t))

        @pl.loop(*span(t))
        def _(g):
            gate_step(1, g, BM)

    def group(t, size):
        c, (low, high), u = t // nd, span(t % nd), nd + 2 * (t - nd)
        down_step(t, c, u, BM, lambda: tick(u))
        gate_step(c + 1, low, size, ticked=u + 1)

        @pl.loop(low + 1, high)
        def _(g):
            gate_step(c + 1, g, size)

    x_load(2, BM).start()
    last = wide * nd

    @pl.loop(nd, last)
    def _(t):
        group(t, BM)

        @pl.when((t % nd == nd - 1) & (t < last - 1))
        def _():
            x_load(t // nd + 2, BM).start()

    x_load(wide + 1, TM).start()

    @pl.loop(last, last + nd)
    def _(t):
        group(t, TM)

    @pl.loop(last + nd, downs)
    def _(t):
        u = edge + t - last - nd
        down_step(t, wide + 1, u, TM, lambda: tick(u))

    for u in range(tiles, tiles + 12):
        tick(u, [n for n in range(6, 0, -1) if u - 2 * n < tiles])


def solution(mesh):
    def step(x, w_gate, w_up, w_down):
        rows, d = x.shape
        ff = w_gate.shape[1]
        dma = pltpu.SemaphoreType.DMA
        return pl.pallas_call(
            kernel,
            out_shape=jax.ShapeDtypeStruct((rows, d), BF16),
            in_specs=[pl.BlockSpec(memory_space=pl.ANY)] * 4,
            out_specs=pl.BlockSpec(memory_space=pl.ANY),
            scratch_shapes=[
                pltpu.VMEM((BM, d), BF16),
                pltpu.VMEM((NW, d, 2 * GC), BF16),
                pltpu.VMEM((2, BM, ff), BF16),
                pltpu.VMEM((2, ff, DC), BF16),
                pltpu.VMEM((NB, H0, DC), F32),
                pltpu.VMEM((NB, H0, DC), BF16),
                pltpu.VMEM((NB, H0, DC), BF16),
                pltpu.VMEM((NB, H1, DC), BF16),
                pltpu.VMEM((NB, H1, DC), BF16),
                pltpu.VMEM((NB, H2, DC), BF16),
                pltpu.VMEM((NB, H2, DC), BF16),
                pltpu.VMEM((NB, H2, DC), BF16),
                dma,
                dma((NW, 2)),
                dma((2,)),
                dma((6, NB)),
                dma((6, NB)),
                dma((NB,)),
            ],
            compiler_params=pltpu.CompilerParams(
                collective_id=0, has_side_effects=True, vmem_limit_bytes=67_043_328
            ),
            cost_estimate=pl.CostEstimate(
                flops=6 * rows * d * ff, bytes_accessed=2 * (rows // BM * 3 * d * ff + 4 * rows * d), transcendentals=rows * ff
            ),
            name="mlp",
        )(x, w_gate, w_up, w_down)

    return jax.shard_map(
        step,
        mesh=mesh,
        in_specs=(P("dp", None), P(None, "tp"), P(None, "tp"), P("tp", None)),
        out_specs=P("dp", None),
        check_vma=False,
    )
```

time: 831 us -> 814 us (0.980)
  Pallas kernels: 797 us -> 779 us
    pallas_call x1, Pallas kernels: 797 us -> 779 us  [step(): pl.pallas_call(kernel, out_shape=jax.ShapeDtypeStruct((rows, d), BF16), i...]
where the time goes in v2:
time: 814 us; the launch traced here: 813 us
  Pallas kernels  779 us (96%)
  local copies, waits for them, and re-layouts  33.7 us (4%)
    pallas_call x1, Pallas kernels, step(): pl.pallas_call(kernel, out_shape=jax.ShapeDtypeStruct((rows, d), BF16), i...  779 us
    unnamed x1, local copies, waits for them, and re-layouts  33.7 us

profile of v2, /device:TPU:0, one launch (start us, length us, event | category | flops | bytes accessed | tf_op | source)
XLA Modules:
  0.0 813.2 jit_solution(1098526019290210823)
XLA Ops:
  0.0 779.5 %mlp.1 = bf16[2048,12288]{1,0:T(8,128)(2,1)} custom-call(bf16[2048,12288]{1,0:T(8,128)(2,1)} %x_hbm.1, bf16[12288,4224]{1,0:T(8,128)(2,1)} %wg_hbm.1, bf16[12288,4224]{1,0:T(8,128)(2,1)} %wu_hbm.1, bf16[4224,12288]{1,0:T(8,128)(2,1)} %wd_hbm.1), custom_call_target="tpu_custom_call" | custom-call | flops 637802643456 | bytes 1447034880 | tf_op jit(solution)/shard_map/mlp/pallas_call | solution.py:238
  779.5 33.7 %copy.6 = bf16[2048,12288]{1,0:T(8,128)(2,1)} copy(bf16[2048,12288]{1,0:T(8,128)(2,1)} %mlp.1) | data formatting | bytes 100663296
